TPU v7x, 32 devices: a whole 2x2x4 slice. The times are simulated.
32 devices in a mesh: dp: 4 (over z), rows: 8 (over y, x, core).
Axes of the slice: x: 2, y: 2, z: 4, core: 2. Of those that a mesh axis runs over, the one named last changes fastest.
Arguments:
- latent: bfloat16 [8, 8, 64, 640], P('dp', 'rows'), may hold values from -16.25 to 16.25
- hidden: bfloat16 [8, 8, 64, 640], P('dp', 'rows'), may hold values from -16.25 to 16.25
- cotangent: bfloat16 [8, 8, 64, 640], P('dp', 'rows'), may hold values from -6 to 6
- filter_one: bfloat16 [9, 640, 640], P(None, 'dp', 'rows'), may hold values from -0.078125 to 0.078125
- filter_two: bfloat16 [9, 640, 640], P(None, 'dp', 'rows'), may hold values from -0.078125 to 0.078125
- gain_one: float32 [640], replicated, may hold values from 0.1 to 1.9
- shift_one: float32 [640], replicated, may hold values from -2.5 to 2.5
- gain_two: float32 [640], replicated, may hold values from 0.1 to 1.9
- shift_two: float32 [640], replicated, may hold values from -2.5 to 2.5
Outputs:
- latent_grad: bfloat16 [8, 8, 64, 640], P('dp', 'rows')
All inputs are finite; a program needn't handle non-finite values.
Results may differ from a plain program's by a relative error of at most 0.0027.
Values may be sent and summed in bfloat16 or wider, within the bound.
A program may use at most 128 MiB of HBM per device.

v0:
```python
import jax
import jax.numpy as jnp
from jax import lax
from jax.sharding import PartitionSpec as P

GROUPS = 16
GSIZE = 40


def extended(block, sides, width):
    for axis, dim in sides:
        count = lax.axis_size(axis)
        forward = [(i, i + 1) for i in range(count - 1)]
        backward = [(target, source) for source, target in forward]
        low = lax.ppermute(
            lax.slice_in_dim(block, block.shape[dim] - width, None, axis=dim), axis, forward
        )
        high = lax.ppermute(lax.slice_in_dim(block, 0, width, axis=dim), axis, backward)
        block = jnp.concatenate([low, block, high], axis=dim)
    return block


def group_sums(values):
    per_channel = jnp.sum(values, axis=(1, 2))
    return jnp.sum(per_channel.reshape(per_channel.shape[0], GROUPS, -1), axis=2)


def expand_groups(moment):
    return jnp.repeat(moment, GSIZE, axis=1)[:, None, None, :]


def finish_stats(sum_plain, sum_square, number):
    average = sum_plain / number
    variance = sum_square / number - average * average
    return (average, lax.rsqrt(variance + 1e-05))


def reduced_stats(field, number):
    values = field.astype(jnp.float32)
    sum_plain, sum_square = lax.psum((group_sums(values), group_sums(values * values)), "rows")
    return finish_stats(sum_plain, sum_square, number)


def norm_backward(field, stats, gain, shift, incoming, number):
    average, inverse = stats
    values = field.astype(jnp.float32)
    normed = (values - expand_groups(average)) * expand_groups(inverse)
    linear = normed * gain + shift
    logistic = jax.nn.sigmoid(linear)
    scaled = incoming * logistic * (1.0 + linear * (1.0 - logistic)) * gain
    sum_first, sum_second = lax.psum((group_sums(scaled), group_sums(scaled * normed)), "rows")
    first = sum_first / number
    second = sum_second / number
    return expand_groups(inverse) * (scaled - expand_groups(first) - normed * expand_groups(second))


def conv_backward(gradient, weights):
    images, rows_here, breadth, channels = gradient.shape
    padded = extended(gradient, (("rows", 1),), 1)
    padded = jnp.pad(padded, ((0, 0), (0, 0), (1, 1), (0, 0)))
    pixels = images * rows_here * breadth
    shifted = []
    for tap_index in range(9):
        down_step = tap_index // 3 - 1
        side_step = tap_index % 3 - 1
        window = padded[
            :, 1 - down_step : 1 - down_step + rows_here, 1 - side_step : 1 - side_step + breadth, :
        ]
        shifted.append(window.reshape(pixels, channels))
    stacked = jnp.stack(shifted, axis=1)
    gathered = lax.all_gather(weights, "dp", axis=1, tiled=True)
    section = lax.all_gather(gathered, "rows", axis=2, tiled=True)
    columns = section.shape[2]
    window = stacked.reshape(pixels, 9 * columns)
    flat = jnp.transpose(section, (0, 2, 1)).reshape(9 * columns, section.shape[1])
    result = jnp.dot(window, flat, preferred_element_type=jnp.float32)
    return result.reshape(images, rows_here, breadth, channels)


def body(
    latent, hidden, cotangent, filter_one, filter_two, gain_one, shift_one, gain_two, shift_two
):
    number = latent.shape[1] * lax.axis_size("rows") * latent.shape[2] * GSIZE
    stats_two = reduced_stats(hidden, number)
    back_two = conv_backward(cotangent, filter_two)
    hidden_grad = norm_backward(hidden, stats_two, gain_two, shift_two, back_two, number).astype(
        jnp.bfloat16
    )
    stats_one = reduced_stats(latent, number)
    back_one = conv_backward(hidden_grad, filter_one)
    latent_part = norm_backward(latent, stats_one, gain_one, shift_one, back_one, number)
    return (cotangent.astype(jnp.float32) + latent_part).astype(jnp.bfloat16)


def solution(mesh):
    in_specs = (
        P("dp", "rows", None, None),
        P("dp", "rows", None, None),
        P("dp", "rows", None, None),
        P(None, "dp", "rows"),
        P(None, "dp", "rows"),
        P(),
        P(),
        P(),
        P(),
    )
    out_specs = P("dp", "rows", None, None)
    return jax.shard_map(body, mesh=mesh, in_specs=in_specs, out_specs=out_specs, check_vma=False)
```

profile of v0, /device:TPU:28, one launch (start us, length us, event | category | flops | bytes accessed | tf_op | source)
XLA Modules:
  0.0 223.1 jit_solution(1200964164859489196)
XLA Ops:
  6.5 1.2 copy.112
  7.7 47.0 %all_gather.12 = bf16[9,640,80]{2,0,1:T(8,128)(2,1)S(1)} all-gather(bf16[9,160,80]{2,0,1:T(8,128)(2,1)S(1)} %copy.112), channel_id=1, replica_groups=mesh['dp'=4,'rows'=8] {'dp'}, dimensions={1}, use_global_device_ids=true | all-gather | bytes 1152000 | tf_op jit(solution)/shard_map/all_gather | solution.py:71
  54.7 3.0 %copy.113 = bf16[9,640,80]{1,2,0:T(8,128)(2,1)} copy(bf16[9,640,80]{2,0,1:T(8,128)(2,1)S(1)} %all_gather.12) | data formatting | bytes 1843200 | tf_op jit(solution)/shard_map/all_gather | solution.py:71
  57.8 0.2 copy.123
  58.0 45.9 %all_gather.14 = bf16[9,640,80]{2,0,1:T(8,128)(2,1)S(1)} all-gather(bf16[9,160,80]{2,0,1:T(8,128)(2,1)S(1)} %copy.123), channel_id=1, replica_groups=mesh['dp'=4,'rows'=8] {'dp'}, dimensions={1}, use_global_device_ids=true | all-gather | bytes 1152000 | tf_op jit(solution)/shard_map/all_gather | solution.py:71
  103.8 3.0 %copy.124 = bf16[9,640,80]{1,2,0:T(8,128)(2,1)} copy(bf16[9,640,80]{2,0,1:T(8,128)(2,1)S(1)} %all_gather.14) | data formatting | bytes 1843200 | tf_op jit(solution)/shard_map/all_gather | solution.py:71
  106.9 2.1 collective-permute-start
  108.9 4.5 %collective-permute-start.1 = (bf16[2,1,64,640]{3,2,1,0:T(8,128)(2,1)S(1)}, bf16[2,1,64,640]{3,2,1,0:T(8,128)(2,1)S(1)}, u32[]{:S(2)}, u32[]{:S(2)}) collective-permute-start(bf16[2,1,64,640]{3,2,1,0:T(8,128)(2,1)S(1)} %copy-done), channel_id=1, source_target_pairs={{1,0},{2,1},{3,2},{4,3},{5,4},{6,5},{7,6},{9,8},{10,9},{11,10},{12... | collective-permute-start | bytes 491528 | tf_op jit(solution)/shard_map/ppermute | solution.py:18
  113.9 12.3 %all-reduce.4 = (f32[2,16]{1,0:T(2,128)S(1)}, f32[2,16]{1,0:T(2,128)S(1)}) all-reduce(f32[2,16]{1,0:T(2,128)S(1)} %reduce_sum.151, f32[2,16]{1,0:T(2,128)S(1)} %reduce_sum.149), channel_id=1, replica_groups=mesh['dp'=4,'rows'=8] {'rows'}, use_global_device_ids=true, to_apply=%region_11.12 | all-reduce | flops 64 | bytes 512 | tf_op jit(solution)/shard_map/psum | solution.py:40
  126.3 0.3 copy.107
  126.6 0.1 mul.122
  126.8 0.1 sub.60
  127.3 0.2 fusion.15
  127.5 0.2 fusion.55
  127.6 0.3 copy.103
  127.9 1.0 copy.105
  128.9 1.0 copy.106
  129.8 1.0 copy.108
  130.8 1.0 copy.109
  131.8 1.0 copy.111
  132.8 1.0 copy.104
  133.8 1.0 copy.110
  134.8 11.1 %stack.6 = bf16[128,9,640]{2,1,0:T(8,128)(2,1)S(1)} concatenate(bf16[128,1,640]{2,1,0:T(2,128)(2,1)S(1)} %copy.103, bf16[128,1,640]{2,1,0:T(2,128)(2,1)} %copy.104, bf16[128,1,640]{2,1,0:T(2,128)(2,1)} %copy.105, bf16[128,1,640]{2,1,0:T(2,128)(2,1)} %copy.106, bf16[128,1,640]{2,1,0:T(2,128)(2,1)S(1)} %copy.107, bf16[128,1,640]{2,1,0:T(2,128)(2,1)} %copy.108, ...), dimensions={1} | concatenate | bytes 2949120 | tf_op jit(solution)/shard_map/stack | solution.py:70
  145.9 1.8 reshape.88
  147.7 5.1 %fusion.53 = (f32[2,640]{1,0:T(2,128)S(1)}, f32[2,640]{1,0:T(2,128)S(1)}, f32[2,1,64,640]{3,2,0,1:T(8,128)S(1)}) fusion(f32[2,640]{1,0:T(2,128)S(1)} %mul.122, f32[2,640]{1,0:T(2,128)S(1)} %sub.60, bf16[2,1,64,640]{3,2,1,0:T(8,128)(2,1)S(1)} %copy-done.4, f32[640]{0:T(1024)S(1)} %copy-done.6, f32[640]{0:T(1024)S(1)} %copy-done.7, ...), kind=kOutput, calls=%fused_computation.73 | convolution fusion | flops 945108480 | bytes 9364480 | tf_op jit(solution)/shard_map/dot_general | solution.py:76
  153.1 12.0 %all-reduce.3 = (f32[2,16]{1,0:T(2,128)S(1)}, f32[2,16]{1,0:T(2,128)S(1)}, f32[2,16]{1,0:T(2,128)S(1)}, f32[2,16]{1,0:T(2,128)S(1)}) all-reduce(f32[2,16]{1,0:T(2,128)S(1)} %reduce_sum.155, f32[2,16]{1,0:T(2,128)S(1)} %reduce_sum.153, f32[2,16]{1,0:T(2,128)S(1)} %reduce_sum.147, ...), channel_id=1, replica_groups=mesh['dp'=4,'rows'=8] {'rows'}, use_global_device_ids=true, to_apply=%region_17.18 | all-reduce | flops 128 | bytes 1024 | tf_op jit(solution)/shard_map/psum | solution.py:51
  165.2 0.1 mul.132
  165.5 1.9 collective-permute-start.2
  167.5 4.7 %collective-permute-start.3 = (bf16[2,1,64,640]{3,2,0,1:T(8,128)(2,1)S(1)}, bf16[2,1,64,640]{3,2,0,1:T(8,128)(2,1)S(1)}, u32[]{:S(2)}, u32[]{:S(2)}) collective-permute-start(bf16[2,1,64,640]{3,2,0,1:T(8,128)(2,1)S(1)} %fusion.50), channel_id=1, source_target_pairs={{1,0},{2,1},{3,2},{4,3},{5,4},{6,5},{7,6},{9,8},{10,9},{11,10},{12... | collective-permute-start | bytes 491528 | tf_op jit(solution)/shard_map/ppermute | solution.py:18
  172.2 0.3 copy.118
  172.7 0.1 sub.68
  172.8 1.2 collective-permute-done.2
  174.0 0.9 collective-permute-done.3
  174.8 0.2 fusion.17
  175.0 0.2 fusion.54
  175.1 0.3 copy.114
  175.4 1.0 copy.116
  176.4 1.0 copy.117
  177.4 1.0 copy.119
  178.4 1.0 copy.120
  179.4 1.0 copy.122
  180.3 1.0 copy.115
  181.3 1.0 copy.121
  182.3 11.0 %stack.7 = bf16[128,9,640]{2,1,0:T(8,128)(2,1)S(1)} concatenate(bf16[128,1,640]{2,1,0:T(2,128)(2,1)S(1)} %copy.114, bf16[128,1,640]{2,1,0:T(2,128)(2,1)} %copy.115, bf16[128,1,640]{2,1,0:T(2,128)(2,1)} %copy.116, bf16[128,1,640]{2,1,0:T(2,128)(2,1)} %copy.117, bf16[128,1,640]{2,1,0:T(2,128)(2,1)S(1)} %copy.118, bf16[128,1,640]{2,1,0:T(2,128)(2,1)} %copy.119, ...), dimensions={1} | concatenate | bytes 2949120 | tf_op jit(solution)/shard_map/stack | solution.py:70
  193.4 1.8 reshape.92
  195.2 4.9 %fusion.52 = (f32[2,640]{1,0:T(2,128)S(1)}, f32[2,640]{1,0:T(2,128)S(1)}, f32[2,1,64,640]{3,2,0,1:T(8,128)S(1)}) fusion(f32[2,640]{1,0:T(2,128)S(1)} %mul.118, f32[2,640]{1,0:T(2,128)S(1)} %sub.68, bf16[2,1,64,640]{3,2,1,0:T(8,128)(2,1)S(1)} %copy-done.2, f32[640]{0:T(1024)S(1)} %copy-done.8, f32[640]{0:T(1024)S(1)} %copy-done.9, ...), kind=kOutput, calls=%fused_computation.72 | convolution fusion | flops 945108480 | bytes 9364480 | tf_op jit(solution)/shard_map/dot_general | solution.py:76
  200.5 14.6 %all-reduce.2 = (f32[2,16]{1,0:T(2,128)S(1)}, f32[2,16]{1,0:T(2,128)S(1)}) all-reduce(f32[2,16]{1,0:T(2,128)S(1)} %reduce_sum.159, f32[2,16]{1,0:T(2,128)S(1)} %reduce_sum.157), channel_id=1, replica_groups=mesh['dp'=4,'rows'=8] {'rows'}, use_global_device_ids=true, to_apply=%region_23.24 | all-reduce | flops 64 | bytes 512 | tf_op jit(solution)/shard_map/psum | solution.py:51
  215.5 0.8 fusion.51
  (64 shorter events, 2.7 us)
Async XLA Ops:
  6.5 141.2 %all-gather.3.cloned.1.call-start = ((), (), s32[]{:S(2)}) async-start(), calls=%async_computation | async-start | bytes 8294400 | tf_op jit(solution)/shard_map/all_gather | solution.py:72
  54.7 3.1 %copy-start.5 = (bf16[9,160,80]{2,1,0:T(8,128)(2,1)S(1)}, bf16[9,160,80]{2,1,0:T(8,128)(2,1)}, u32[]{:S(2)}) copy-start(bf16[9,160,80]{2,1,0:T(8,128)(2,1)} %param.12) | copy-start | bytes 691204
  57.7 137.5 %all-gather.5.cloned.1.call-start = ((), (), s32[]{:S(2)}) async-start(), calls=%async_computation.1 | async-start | bytes 8294400 | tf_op jit(solution)/shard_map/all_gather | solution.py:72
  103.8 3.0 %copy-start = (bf16[2,1,64,640]{3,2,1,0:T(8,128)(2,1)S(1)}, bf16[2,1,64,640]{3,2,1,0:T(8,128)(2,1)}, u32[]{:S(2)}) copy-start(bf16[2,1,64,640]{3,2,1,0:T(8,128)(2,1)} %param.11) | copy-start | bytes 491524
  103.8 9.6 %copy-start.3 = (bf16[2,1,64,640]{3,2,1,0:T(8,128)(2,1)S(1)}, bf16[2,1,64,640]{3,2,1,0:T(8,128)(2,1)}, u32[]{:S(2)}) copy-start(bf16[2,1,64,640]{3,2,1,0:T(8,128)(2,1)} %param.10) | copy-start | bytes 491524
  106.8 20.0 %copy-start.1 = (bf16[2,1,64,640]{3,2,1,0:T(8,128)(2,1)S(1)}, bf16[2,1,64,640]{3,2,1,0:T(8,128)(2,1)}, u32[]{:S(2)}) copy-start(bf16[2,1,64,640]{3,2,1,0:T(8,128)(2,1)} %param.9) | copy-start | bytes 491524
  106.9 20.4 %collective-permute-start = (bf16[2,1,64,640]{3,2,1,0:T(8,128)(2,1)S(1)}, bf16[2,1,64,640]{3,2,1,0:T(8,128)(2,1)S(1)}, u32[]{:S(2)}, u32[]{:S(2)}) collective-permute-start(bf16[2,1,64,640]{3,2,1,0:T(8,128)(2,1)S(1)} %copy-done), channel_id=1, source_target_pairs={{0,1},{1,2},{2,3},{3,4},{4,5},{5,6},{6,7},{8,9},{9,10},{10,11},{11... | collective-permute-start | bytes 491528 | tf_op jit(solution)/shard_map/ppermute | solution.py:15
  108.9 18.4 %collective-permute-start.1 = (bf16[2,1,64,640]{3,2,1,0:T(8,128)(2,1)S(1)}, bf16[2,1,64,640]{3,2,1,0:T(8,128)(2,1)S(1)}, u32[]{:S(2)}, u32[]{:S(2)}) collective-permute-start(bf16[2,1,64,640]{3,2,1,0:T(8,128)(2,1)S(1)} %copy-done), channel_id=1, source_target_pairs={{1,0},{2,1},{3,2},{4,3},{5,4},{6,5},{7,6},{9,8},{10,9},{11,10},{12... | collective-permute-start | bytes 491528 | tf_op jit(solution)/shard_map/ppermute | solution.py:18
  145.9 1.8 copy-start.4
  145.9 1.8 copy-start.6
  145.9 1.8 copy-start.7
  165.5 8.4 %collective-permute-start.2 = (bf16[2,1,64,640]{3,2,0,1:T(8,128)(2,1)S(1)}, bf16[2,1,64,640]{3,2,0,1:T(8,128)(2,1)S(1)}, u32[]{:S(2)}, u32[]{:S(2)}) collective-permute-start(bf16[2,1,64,640]{3,2,0,1:T(8,128)(2,1)S(1)} %fusion.50), channel_id=1, source_target_pairs={{0,1},{1,2},{2,3},{3,4},{4,5},{5,6},{6,7},{8,9},{9,10},{10,11},{11... | collective-permute-start | bytes 491528 | tf_op jit(solution)/shard_map/ppermute | solution.py:15
  167.5 7.4 %collective-permute-start.3 = (bf16[2,1,64,640]{3,2,0,1:T(8,128)(2,1)S(1)}, bf16[2,1,64,640]{3,2,0,1:T(8,128)(2,1)S(1)}, u32[]{:S(2)}, u32[]{:S(2)}) collective-permute-start(bf16[2,1,64,640]{3,2,0,1:T(8,128)(2,1)S(1)} %fusion.50), channel_id=1, source_target_pairs={{1,0},{2,1},{3,2},{4,3},{5,4},{6,5},{7,6},{9,8},{10,9},{11,10},{12... | collective-permute-start | bytes 491528 | tf_op jit(solution)/shard_map/ppermute | solution.py:18
  193.4 1.8 copy-start.2
  193.4 1.8 copy-start.8
  193.4 1.8 copy-start.9
Sparse Core Ops, SparseCore 0:
  57.9 50.5 all-gather.2
  110.4 50.1 all-gather.4
where the time goes:
time: 225 us; the launch traced here: 223 us
  blocking collectives  132 us (59%)
  local copies, waits for them, and re-layouts  50.2 us (22%)
  between operations  13.8 us (6%)
  starting transfers between devices  13.3 us (6%)
  matrix products  10 us (4%)
    all_gather x2, blocking collectives, conv_backward(): gathered = lax.all_gather(weights, 'dp', axis=1, tiled=True)  92.9 us
    another operation x20, local copies, waits for them, and re-layouts, conv_backward(): stacked = jnp.stack(shifted, axis=1)  36.9 us
    psum x2, blocking collectives, norm_backward(): lax.psum((group_sums(scaled), group_sums(scaled * normed)), 'rows')  26.5 us
    psum x1, blocking collectives, reduced_stats(): lax.psum((group_sums(values), group_sums(values * values)), 'rows')  12.3 us
    dot_general x2, matrix products, conv_backward(): result = jnp.dot(window, flat, preferred_element_type=jnp.float32)  10 us
    ppermute x2, starting transfers between devices, extended(): lax.ppermute(lax.slice_in_dim(block, 0, width, axis=dim), axis, backward)  9.26 us
    all_gather x2, local copies, waits for them, and re-layouts, conv_backward(): gathered = lax.all_gather(weights, 'dp', axis=1, tiled=True)  5.97 us
  transfers between devices with their start and end apart: 6, of which 2 were waited for; matrix products, arithmetic and copies ran while one was open for 23% of the time, Pallas kernels for 0%

commit v1 on v0

--- a/solution.py
+++ b/solution.py
@@ -69,7 +69,9 @@
         shifted.append(window.reshape(pixels, channels))
     stacked = jnp.stack(shifted, axis=1)
     gathered = lax.all_gather(weights, "dp", axis=1, tiled=True)
-    section = lax.all_gather(gathered, "rows", axis=2, tiled=True)
+    section = jnp.concatenate(
+        lax.all_to_all(jnp.stack([gathered] * lax.axis_size("rows")), "rows", 0, 0), axis=2
+    )
     columns = section.shape[2]
     window = stacked.reshape(pixels, 9 * columns)
     flat = jnp.transpose(section, (0, 2, 1)).reshape(9 * columns, section.shape[1])

time: 225 us -> 318 us (1.41)
  waiting for transfers between devices: 2.08 us -> 51.5 us
  blocking collectives: 132 us -> 167 us
  between operations: 13.8 us -> 0.37 us
  local copies, waits for them, and re-layouts: 50.2 us -> 63.6 us
  starting transfers between devices: 13.3 us -> 24.8 us
  matrix products: 10 us -> 6.34 us
    psum x1, blocking collectives: 12.3 us -> 85.9 us  [reduced_stats(): lax.psum((group_sums(values), group_sums(values * values)), 'rows')]
    all_to_all x0 -> x2, waiting for transfers between devices: none -> 51.5 us  [conv_backward(): lax.all_to_all(jnp.stack([gathered] * lax.axis_size('rows')), 'rows', 0, 0)]
    all_gather x2, blocking collectives: 92.9 us -> 57.6 us  [conv_backward(): gathered = lax.all_gather(weights, 'dp', axis=1, tiled=True)]
    all_to_all x0 -> x2, starting transfers between devices: none -> 11.8 us  [conv_backward(): lax.all_to_all(jnp.stack([gathered] * lax.axis_size('rows')), 'rows', 0, 0)]
    all_to_all x0 -> x2, local copies, waits for them, and re-layouts: none -> 10.9 us  [conv_backward(): lax.all_to_all(jnp.stack([gathered] * lax.axis_size('rows')), 'rows', 0, 0)]
    another operation x2 -> x4, local copies, waits for them, and re-layouts: 3.57 us -> 10.6 us  [the longest x2 7.04 us: conv_backward(): jnp.stack([gathered] * lax.axis_size('rows'))]
    dot_general x2, matrix products: 10 us -> 6.34 us  [conv_backward(): result = jnp.dot(window, flat, preferred_element_type=jnp.float32)]
  transfers between devices with their start and end apart: 6 -> 6, of which waited for: 2 -> 1; matrix products, arithmetic and copies ran while one was open for 23% -> 12% of each run, Pallas kernels for 0% -> 0%
where the time goes in v1:
time: 318 us; the launch traced here: 316 us
  blocking collectives  167 us (53%)
  local copies, waits for them, and re-layouts  63.6 us (20%)
  waiting for transfers between devices  51.5 us (16%)
  starting transfers between devices  24.8 us (8%)
  matrix products  6.34 us (2%)
    psum x1, blocking collectives, reduced_stats(): lax.psum((group_sums(values), group_sums(values * values)), 'rows')  85.9 us
    all_gather x2, blocking collectives, conv_backward(): gathered = lax.all_gather(weights, 'dp', axis=1, tiled=True)  57.6 us
    all_to_all x2, waiting for transfers between devices, conv_backward(): lax.all_to_all(jnp.stack([gathered] * lax.axis_size('rows')), 'rows', 0, 0)  51.5 us
    another operation x20, local copies, waits for them, and re-layouts, conv_backward(): stacked = jnp.stack(shifted, axis=1)  36.9 us
    psum x2, blocking collectives, norm_backward(): lax.psum((group_sums(scaled), group_sums(scaled * normed)), 'rows')  23.6 us
    all_to_all x2, starting transfers between devices, conv_backward(): lax.all_to_all(jnp.stack([gathered] * lax.axis_size('rows')), 'rows', 0, 0)  11.8 us
    all_to_all x2, local copies, waits for them, and re-layouts, conv_backward(): lax.all_to_all(jnp.stack([gathered] * lax.axis_size('rows')), 'rows', 0, 0)  10.9 us
    ppermute x2, starting transfers between devices, extended(): lax.ppermute(lax.slice_in_dim(block, 0, width, axis=dim), axis, backward)  9.15 us
  transfers between devices with their start and end apart: 6, of which 1 were waited for; matrix products, arithmetic and copies ran while one was open for 12% of the time, Pallas kernels for 0%

profile of v1, /device:TPU:28, one launch (start us, length us, event | category | flops | bytes accessed | tf_op | source)
XLA Modules:
  0.0 315.8 jit_solution(11389577183265836140)
XLA Ops:
  0.0 28.8 %all_gather.6 = bf16[9,640,80]{2,1,0:T(8,128)(2,1)S(1)} all-gather(bf16[9,160,80]{2,1,0:T(8,128)(2,1)} %param.13), channel_id=1, replica_groups=mesh['dp'=4,'rows'=8] {'dp'}, dimensions={1}, use_global_device_ids=true | all-gather | bytes 1152000 | tf_op jit(solution)/shard_map/all_gather | solution.py:71
  28.8 1.5 copy.112
  30.2 3.5 %stack.9 = bf16[8,9,640,80]{2,3,1,0:T(8,128)(2,1)} broadcast(bf16[9,640,80]{1,2,0:T(8,128)(2,1)S(1)} %copy.112), dimensions={1,2,3} | broadcast | bytes 8294400 | tf_op jit(solution)/shard_map/stack | solution.py:73
  33.8 5.4 %all-to-all-start = ((bf16[8,9,640,80]{2,3,1,0:T(8,128)(2,1)}), bf16[8,9,640,80]{2,3,1,0:T(8,128)(2,1)}, u32[]{:S(2)}, u32[]{:S(2)}) async-start(bf16[8,9,640,80]{2,3,1,0:T(8,128)(2,1)} %stack.9), calls=%async_computation | async-start | bytes 14745600 | tf_op jit(solution)/shard_map/all_to_all | solution.py:73
  39.2 28.8 %all_gather.7 = bf16[9,640,80]{2,1,0:T(8,128)(2,1)S(1)} all-gather(bf16[9,160,80]{2,1,0:T(8,128)(2,1)S(1)} %copy-done.6), channel_id=1, replica_groups=mesh['dp'=4,'rows'=8] {'dp'}, dimensions={1}, use_global_device_ids=true | all-gather | bytes 1152000 | tf_op jit(solution)/shard_map/all_gather | solution.py:71
  68.0 1.5 copy.123
  69.5 51.5 %all-to-all-done = bf16[8,9,640,80]{2,3,1,0:T(8,128)(2,1)} async-done(((bf16[8,9,640,80]{2,3,1,0:T(8,128)(2,1)}), bf16[8,9,640,80]{2,3,1,0:T(8,128)(2,1)}, u32[]{:S(2)}, u32[]{:S(2)}) %all-to-all-start) | async-done | bytes 7372832 | tf_op jit(solution)/shard_map/all_to_all | solution.py:73
  120.9 3.5 %stack.11 = bf16[8,9,640,80]{2,3,1,0:T(8,128)(2,1)} broadcast(bf16[9,640,80]{1,2,0:T(8,128)(2,1)S(1)} %copy.123), dimensions={1,2,3} | broadcast | bytes 8294400 | tf_op jit(solution)/shard_map/stack | solution.py:73
  124.5 6.4 %all-to-all-start.1 = ((bf16[8,9,640,80]{2,3,1,0:T(8,128)(2,1)}), bf16[8,9,640,80]{2,3,1,0:T(8,128)(2,1)}, u32[]{:S(2)}, u32[]{:S(2)}) async-start(bf16[8,9,640,80]{2,3,1,0:T(8,128)(2,1)} %stack.11), calls=%async_computation.1 | async-start | bytes 14745600 | tf_op jit(solution)/shard_map/all_to_all | solution.py:73
  130.8 2.0 collective-permute-start
  132.9 4.4 %collective-permute-start.1 = (bf16[2,1,64,640]{3,2,1,0:T(8,128)(2,1)S(1)}, bf16[2,1,64,640]{3,2,1,0:T(8,128)(2,1)S(1)}, u32[]{:S(2)}, u32[]{:S(2)}) collective-permute-start(bf16[2,1,64,640]{3,2,1,0:T(8,128)(2,1)S(1)} %copy-done), channel_id=1, source_target_pairs={{1,0},{2,1},{3,2},{4,3},{5,4},{6,5},{7,6},{9,8},{10,9},{11,10},{12... | collective-permute-start | bytes 491528 | tf_op jit(solution)/shard_map/ppermute | solution.py:18
  137.7 85.9 %all-reduce.4 = (f32[2,16]{1,0:T(2,128)S(1)}, f32[2,16]{1,0:T(2,128)S(1)}) all-reduce(f32[2,16]{1,0:T(2,128)S(1)} %reduce_sum.151, f32[2,16]{1,0:T(2,128)S(1)} %reduce_sum.149), channel_id=1, replica_groups=mesh['dp'=4,'rows'=8] {'rows'}, use_global_device_ids=true, to_apply=%region_11.12 | all-reduce | flops 64 | bytes 512 | tf_op jit(solution)/shard_map/psum | solution.py:40
  223.6 0.3 copy.107
  224.7 0.2 fusion.15
  224.8 0.2 fusion.55
  225.0 0.3 copy.103
  225.2 1.0 copy.105
  226.2 1.0 copy.106
  227.2 1.0 copy.108
  228.2 1.0 copy.109
  229.2 1.0 copy.111
  230.2 1.0 copy.104
  231.2 1.0 copy.110
  232.2 11.1 %stack.8 = bf16[128,9,640]{2,1,0:T(8,128)(2,1)S(1)} concatenate(bf16[128,1,640]{2,1,0:T(2,128)(2,1)S(1)} %copy.103, bf16[128,1,640]{2,1,0:T(2,128)(2,1)} %copy.104, bf16[128,1,640]{2,1,0:T(2,128)(2,1)} %copy.105, bf16[128,1,640]{2,1,0:T(2,128)(2,1)} %copy.106, bf16[128,1,640]{2,1,0:T(2,128)(2,1)S(1)} %copy.107, bf16[128,1,640]{2,1,0:T(2,128)(2,1)} %copy.108, ...), dimensions={1} | concatenate | bytes 2949120 | tf_op jit(solution)/shard_map/stack | solution.py:70
  243.2 1.8 reshape.104
  245.0 4.0 %copy.113 = bf16[8,9,640,80]{2,3,0,1:T(8,128)(2,1)S(1)} copy(bf16[8,9,640,80]{2,3,1,0:T(8,128)(2,1)} %all-to-all-done) | data formatting | bytes 14745600 | tf_op jit(solution)/shard_map/all_to_all | solution.py:73
  249.1 1.4 fusion.53
  250.8 11.8 %all-reduce.3 = (f32[2,16]{1,0:T(2,128)S(1)}, f32[2,16]{1,0:T(2,128)S(1)}, f32[2,16]{1,0:T(2,128)S(1)}, f32[2,16]{1,0:T(2,128)S(1)}) all-reduce(f32[2,16]{1,0:T(2,128)S(1)} %reduce_sum.155, f32[2,16]{1,0:T(2,128)S(1)} %reduce_sum.153, f32[2,16]{1,0:T(2,128)S(1)} %reduce_sum.147, ...), channel_id=1, replica_groups=mesh['dp'=4,'rows'=8] {'rows'}, use_global_device_ids=true, to_apply=%region_17.18 | all-reduce | flops 128 | bytes 1024 | tf_op jit(solution)/shard_map/psum | solution.py:51
  262.7 0.1 mul.132
  263.1 1.9 collective-permute-start.2
  265.0 4.7 %collective-permute-start.3 = (bf16[2,1,64,640]{3,2,0,1:T(8,128)(2,1)S(1)}, bf16[2,1,64,640]{3,2,0,1:T(8,128)(2,1)S(1)}, u32[]{:S(2)}, u32[]{:S(2)}) collective-permute-start(bf16[2,1,64,640]{3,2,0,1:T(8,128)(2,1)S(1)} %fusion.50), channel_id=1, source_target_pairs={{1,0},{2,1},{3,2},{4,3},{5,4},{6,5},{7,6},{9,8},{10,9},{11,10},{12... | collective-permute-start | bytes 491528 | tf_op jit(solution)/shard_map/ppermute | solution.py:18
  269.7 0.3 copy.118
  270.4 6.9 %copy.124 = bf16[8,9,640,80]{2,3,0,1:T(8,128)(2,1)} copy(bf16[8,9,640,80]{2,3,1,0:T(8,128)(2,1)} %all-to-all-done.1) | data formatting | bytes 14745600 | tf_op jit(solution)/shard_map/all_to_all | solution.py:73
  277.3 0.2 fusion.17
  277.4 0.2 fusion.54
  277.6 0.3 copy.114
  277.9 1.0 copy.116
  278.8 1.0 copy.117
  279.8 1.0 copy.119
  280.8 1.0 copy.120
  281.8 1.0 copy.122
  282.8 1.0 copy.115
  283.8 1.0 copy.121
  284.7 11.0 %stack.10 = bf16[128,9,640]{2,1,0:T(8,128)(2,1)S(1)} concatenate(bf16[128,1,640]{2,1,0:T(2,128)(2,1)S(1)} %copy.114, bf16[128,1,640]{2,1,0:T(2,128)(2,1)} %copy.115, bf16[128,1,640]{2,1,0:T(2,128)(2,1)} %copy.116, bf16[128,1,640]{2,1,0:T(2,128)(2,1)} %copy.117, bf16[128,1,640]{2,1,0:T(2,128)(2,1)S(1)} %copy.118, bf16[128,1,640]{2,1,0:T(2,128)(2,1)} %copy.119, ...), dimensions={1} | concatenate | bytes 2949120 | tf_op jit(solution)/shard_map/stack | solution.py:70
  295.8 1.7 reshape.110
  297.6 4.9 %fusion.52 = (f32[2,640]{1,0:T(2,128)S(1)}, f32[2,640]{1,0:T(2,128)S(1)}, f32[2,1,64,640]{3,2,0,1:T(8,128)S(1)}) fusion(f32[2,640]{1,0:T(2,128)S(1)} %mul.118, f32[2,640]{1,0:T(2,128)S(1)} %sub.68, bf16[2,1,64,640]{3,2,1,0:T(8,128)(2,1)S(1)} %copy-done.3, f32[640]{0:T(1024)S(1)} %copy-done.9, f32[640]{0:T(1024)S(1)} %copy-done.10, ...), kind=kOutput, calls=%fused_computation.72 | convolution fusion | flops 945108480 | bytes 9364480 | tf_op jit(solution)/shard_map/dot_general | solution.py:78
  302.9 11.8 %all-reduce.2 = (f32[2,16]{1,0:T(2,128)S(1)}, f32[2,16]{1,0:T(2,128)S(1)}) all-reduce(f32[2,16]{1,0:T(2,128)S(1)} %reduce_sum.159, f32[2,16]{1,0:T(2,128)S(1)} %reduce_sum.157), channel_id=1, replica_groups=mesh['dp'=4,'rows'=8] {'rows'}, use_global_device_ids=true, to_apply=%region_23.24 | all-reduce | flops 64 | bytes 512 | tf_op jit(solution)/shard_map/psum | solution.py:51
  315.0 0.8 fusion.51
  (66 shorter events, 2.9 us)
Async XLA Ops:
  33.8 5.4 %copy-start.6 = (bf16[9,160,80]{2,1,0:T(8,128)(2,1)S(1)}, bf16[9,160,80]{2,1,0:T(8,128)(2,1)}, u32[]{:S(2)}) copy-start(bf16[9,160,80]{2,1,0:T(8,128)(2,1)} %param.12) | copy-start | bytes 691204
  33.8 87.2 %all-to-all-start = ((bf16[8,9,640,80]{2,3,1,0:T(8,128)(2,1)}), bf16[8,9,640,80]{2,3,1,0:T(8,128)(2,1)}, u32[]{:S(2)}, u32[]{:S(2)}) async-start(bf16[8,9,640,80]{2,3,1,0:T(8,128)(2,1)} %stack.9), calls=%async_computation | async-start | bytes 14745600 | tf_op jit(solution)/shard_map/all_to_all | solution.py:73
  124.5 6.4 %copy-start = (bf16[2,1,64,640]{3,2,1,0:T(8,128)(2,1)S(1)}, bf16[2,1,64,640]{3,2,1,0:T(8,128)(2,1)}, u32[]{:S(2)}) copy-start(bf16[2,1,64,640]{3,2,1,0:T(8,128)(2,1)} %param.11) | copy-start | bytes 491524
  124.5 12.8 %copy-start.4 = (bf16[2,1,64,640]{3,2,1,0:T(8,128)(2,1)S(1)}, bf16[2,1,64,640]{3,2,1,0:T(8,128)(2,1)}, u32[]{:S(2)}) copy-start(bf16[2,1,64,640]{3,2,1,0:T(8,128)(2,1)} %param.10) | copy-start | bytes 491524
  124.5 99.8 %copy-start.2 = (bf16[2,1,64,640]{3,2,1,0:T(8,128)(2,1)S(1)}, bf16[2,1,64,640]{3,2,1,0:T(8,128)(2,1)}, u32[]{:S(2)}) copy-start(bf16[2,1,64,640]{3,2,1,0:T(8,128)(2,1)} %param.9) | copy-start | bytes 491524
  124.5 145.9 %all-to-all-start.1 = ((bf16[8,9,640,80]{2,3,1,0:T(8,128)(2,1)}), bf16[8,9,640,80]{2,3,1,0:T(8,128)(2,1)}, u32[]{:S(2)}, u32[]{:S(2)}) async-start(bf16[8,9,640,80]{2,3,1,0:T(8,128)(2,1)} %stack.11), calls=%async_computation.1 | async-start | bytes 14745600 | tf_op jit(solution)/shard_map/all_to_all | solution.py:73
  130.8 93.8 %collective-permute-start = (bf16[2,1,64,640]{3,2,1,0:T(8,128)(2,1)S(1)}, bf16[2,1,64,640]{3,2,1,0:T(8,128)(2,1)S(1)}, u32[]{:S(2)}, u32[]{:S(2)}) collective-permute-start(bf16[2,1,64,640]{3,2,1,0:T(8,128)(2,1)S(1)} %copy-done), channel_id=1, source_target_pairs={{0,1},{1,2},{2,3},{3,4},{4,5},{5,6},{6,7},{8,9},{9,10},{10,11},{11... | collective-permute-start | bytes 491528 | tf_op jit(solution)/shard_map/ppermute | solution.py:15
  132.9 91.8 %collective-permute-start.1 = (bf16[2,1,64,640]{3,2,1,0:T(8,128)(2,1)S(1)}, bf16[2,1,64,640]{3,2,1,0:T(8,128)(2,1)S(1)}, u32[]{:S(2)}, u32[]{:S(2)}) collective-permute-start(bf16[2,1,64,640]{3,2,1,0:T(8,128)(2,1)S(1)} %copy-done), channel_id=1, source_target_pairs={{1,0},{2,1},{3,2},{4,3},{5,4},{6,5},{7,6},{9,8},{10,9},{11,10},{12... | collective-permute-start | bytes 491528 | tf_op jit(solution)/shard_map/ppermute | solution.py:18
  245.0 4.0 %copy-start.1 = (bf16[2,64,5760]{2,1,0:T(8,128)(2,1)S(1)}, bf16[2,64,5760]{2,1,0:T(8,128)(2,1)}, u32[]{:S(2)}) copy-start(bf16[2,64,5760]{2,1,0:T(8,128)(2,1)} %reshape.104) | copy-start | bytes 4423684
  245.0 4.0 %copy-start.5 = (bf16[2,1,64,640]{3,2,1,0:T(8,128)(2,1)S(1)}, bf16[2,1,64,640]{3,2,1,0:T(8,128)(2,1)}, u32[]{:S(2)}) copy-start(bf16[2,1,64,640]{3,2,1,0:T(8,128)(2,1)} %param.10) | copy-start | bytes 491524
  245.0 4.0 %copy-start.7 = (f32[640]{0:T(1024)S(1)}, f32[640]{0:T(1024)}, u32[]{:S(2)}) copy-start(f32[640]{0:T(1024)} %param.17) | copy-start | bytes 7684
  245.0 4.1 %copy-start.8 = (f32[640]{0:T(1024)S(1)}, f32[640]{0:T(1024)}, u32[]{:S(2)}) copy-start(f32[640]{0:T(1024)} %param.16) | copy-start | bytes 7684
  263.1 14.2 %collective-permute-start.2 = (bf16[2,1,64,640]{3,2,0,1:T(8,128)(2,1)S(1)}, bf16[2,1,64,640]{3,2,0,1:T(8,128)(2,1)S(1)}, u32[]{:S(2)}, u32[]{:S(2)}) collective-permute-start(bf16[2,1,64,640]{3,2,0,1:T(8,128)(2,1)S(1)} %fusion.50), channel_id=1, source_target_pairs={{0,1},{1,2},{2,3},{3,4},{4,5},{5,6},{6,7},{8,9},{9,10},{10,11},{11... | collective-permute-start | bytes 491528 | tf_op jit(solution)/shard_map/ppermute | solution.py:15
  265.0 12.2 %collective-permute-start.3 = (bf16[2,1,64,640]{3,2,0,1:T(8,128)(2,1)S(1)}, bf16[2,1,64,640]{3,2,0,1:T(8,128)(2,1)S(1)}, u32[]{:S(2)}, u32[]{:S(2)}) collective-permute-start(bf16[2,1,64,640]{3,2,0,1:T(8,128)(2,1)S(1)} %fusion.50), channel_id=1, source_target_pairs={{1,0},{2,1},{3,2},{4,3},{5,4},{6,5},{7,6},{9,8},{10,9},{11,10},{12... | collective-permute-start | bytes 491528 | tf_op jit(solution)/shard_map/ppermute | solution.py:18
  295.8 1.8 copy-start.3
  295.8 1.8 copy-start.9
  295.8 1.8 copy-start.10
